TPU v7x, 128 devices: a whole 4x4x4 slice. The times are simulated.
128 devices in a mesh: blk: 64 (over z_lo, x, y, core), grp: 2 (over z_hi).
Axes of the slice: x: 4, y: 4, z: 4 (z_hi: 2, z_lo: 2; z = z_hi * 2 + z_lo), core: 2. Of those that a mesh axis runs over, the one named last changes fastest.
Arguments:
- returns: float32 [512, 32768], P(None, ('blk', 'grp')), may hold values from -200 to 200
Outputs:
- correlation: bfloat16 [32768, 32768], P(('blk', 'grp'))
All inputs are finite; a program needn't handle non-finite values.
Results may differ from a plain program's by a relative error of at most 0.0034.
Values may be sent and summed in bfloat16 or wider, within the bound.
A program may use at most 128 MiB of HBM per device.

v0:
```python
import math
import jax
import jax.numpy as jnp
from jax import lax
from jax.sharding import Mesh
from jax.sharding import PartitionSpec as P

BLK_GRP = ("blk_0", "blk_1", "blk_2", "blk_3", "grp")


def by_axis(array, axes):
    for axis in axes:
        array = lax.psum(array, axis)
    return array


def gram_tile(first, second):
    return lax.dot_general(
        first, second, (((0,), (0,)), ((), ())), preferred_element_type=jnp.float32
    )


def shards(returns):
    bar_count = returns.shape[0]
    series_dev = returns.shape[1]
    devices = lax.axis_size(BLK_GRP)
    my_index = lax.axis_index(BLK_GRP)
    summed = by_axis(jnp.sum(returns, axis=1), BLK_GRP)
    market = summed / (series_dev * devices)
    excess = returns - market[:, None]
    deviation = excess - jnp.mean(excess, axis=0, keepdims=True)
    inverse = lax.rsqrt(jnp.mean(deviation * deviation, axis=0, keepdims=True) + 1e-06) / math.sqrt(
        bar_count
    )
    zscores = (deviation * inverse).astype(jnp.bfloat16)
    piece = lax.all_gather(zscores, BLK_GRP, axis=1, tiled=True)
    products = gram_tile(zscores, piece)
    column_block = jnp.arange(piece.shape[1], dtype=jnp.int32) // series_dev
    return jnp.where(column_block[None, :] >= my_index, products, jnp.float32(0.0)).astype(
        jnp.bfloat16
    )


def solution(mesh):
    split = Mesh(
        mesh.devices.reshape(2, 4, 4, 2, mesh.shape["grp"]),
        ("blk_0", "blk_1", "blk_2", "blk_3", "grp"),
    )
    in_specs = (P(None, BLK_GRP),)
    out_specs = P(BLK_GRP, None)
    return jax.shard_map(
        shards, mesh=split, in_specs=in_specs, out_specs=out_specs, check_vma=False
    )
```

profile of v0, /device:TPU:1, one launch (start us, length us, event | category | flops | bytes accessed | tf_op | source)
XLA Modules:
  0.0 429.9 jit_solution(4869989052520204716)
XLA Ops:
  6.5 0.0 all-gather.2.cloned.1.call-start
  6.5 1.2 reduce_sum.27
  7.7 4.8 %psum.35 = f32[512]{0:T(512)S(1)} all-reduce(f32[512]{0:T(512)S(1)} %reduce_sum.27), channel_id=1, replica_groups=mesh['blk_0'=2,'blk_1'=4,'blk_2'=4,'blk_3'=2,'grp'=2] {'blk_0'}, use_global_device_ids=true, to_apply=%region_1.0 | all-reduce | flops 512 | bytes 4096 | tf_op jit(solution)/shard_map/psum | solution.py:13
  12.5 8.4 %psum.36 = f32[512]{0:T(512)S(1)} all-reduce(f32[512]{0:T(512)S(1)} %psum.35), channel_id=1, replica_groups=mesh['blk_0'=2,'blk_1'=4,'blk_2'=4,'blk_3'=2,'grp'=2] {'blk_1'}, use_global_device_ids=true, to_apply=%region_2.0 | all-reduce | flops 512 | bytes 4096 | tf_op jit(solution)/shard_map/psum | solution.py:13
  20.9 8.7 %psum.37 = f32[512]{0:T(512)S(1)} all-reduce(f32[512]{0:T(512)S(1)} %psum.36), channel_id=1, replica_groups=mesh['blk_0'=2,'blk_1'=4,'blk_2'=4,'blk_3'=2,'grp'=2] {'blk_2'}, use_global_device_ids=true, to_apply=%region_3.0 | all-reduce | flops 512 | bytes 4096 | tf_op jit(solution)/shard_map/psum | solution.py:13
  29.6 7.8 %psum.38 = f32[512]{0:T(512)S(1)} all-reduce(f32[512]{0:T(512)S(1)} %psum.37), channel_id=1, replica_groups=mesh['blk_0'=2,'blk_1'=4,'blk_2'=4,'blk_3'=2,'grp'=2] {'blk_3'}, use_global_device_ids=true, to_apply=%region_4.0 | all-reduce | flops 512 | bytes 4096 | tf_op jit(solution)/shard_map/psum | solution.py:13
  37.4 5.9 %psum.39 = f32[512]{0:T(512)S(1)} all-reduce(f32[512]{0:T(512)S(1)} %psum.38), channel_id=1, replica_groups=mesh['blk_0'=2,'blk_1'=4,'blk_2'=4,'blk_3'=2,'grp'=2] {'grp'}, use_global_device_ids=true, to_apply=%region_5.0 | all-reduce | flops 512 | bytes 4096 | tf_op jit(solution)/shard_map/psum | solution.py:13
  43.3 1.2 subtract_reduce_fusion
  44.5 1.2 multiply_reduce_fusion
  45.7 1.9 multiply_convert_fusion
  47.6 0.0 all-gather.2.cloned.1.call-update
  47.7 354.2 %all-gather.2.cloned.1.call-done = bf16[512,32768]{1,0:T(8,128)(2,1)} async-done(((bf16[512,256]{1,0:T(8,128)(2,1)}), bf16[512,32768]{1,0:T(8,128)(2,1)}) %all-gather.2.cloned.1.call-update) | async-done | bytes 33554448 | tf_op jit(solution)/shard_map/all_gather | solution.py:36
  401.9 21.2 %fusion = bf16[256,32768]{1,0:T(8,128)(2,1)} fusion(bf16[512,256]{1,0:T(8,128)(2,1)} %multiply_convert_fusion, bf16[512,32768]{1,0:T(8,128)(2,1)} %all-gather.2.cloned.1.call-done, pred[32768]{0:T(1024)(128)(4,1)S(1)} %fusion.1), kind=kOutput, calls=%fused_computation.1 | convolution fusion | flops 8606711808 | bytes 50626560 | tf_op jit(solution)/shard_map/dot_general | solution.py:18
  (4 shorter events, 0.1 us)
Async XLA Ops:
  6.5 395.3 %all-gather.2.cloned.1.call-start = ((), (), s32[]{:S(2)}) async-start(), calls=%async_computation | async-start | bytes 33816576 | tf_op jit(solution)/shard_map/all_gather | solution.py:36
Sparse Core Ops, SparseCore 0:
  47.8 354.0 all-gather.1
where the time goes:
time: 430 us
  waiting for transfers between devices  354 us (82%)
  blocking collectives  35.6 us (8%)
  matrix products  21.2 us (5%)
  between operations  13.4 us (3%)
  other arithmetic  5.51 us (1%)
    all_gather x1, waiting for transfers between devices, shards(): piece = lax.all_gather(zscores, BLK_GRP, axis=1, tiled=True)  354 us
    psum x5, blocking collectives, by_axis(): array = lax.psum(array, axis)  35.6 us
    dot_general x1, matrix products, gram_tile(): lax.dot_general(first, second, (((0,), (0,)), ((), ())), preferred_elemen...  21.2 us
  transfers between devices with their start and end apart: 1, of which 1 were waited for; matrix products, arithmetic and copies ran while one was open for 0% of the time, Pallas kernels for 0%

commit v1 on v0

--- a/solution.py
+++ b/solution.py
@@ -1,3 +1,4 @@
+import functools
 import math
 import jax
 import jax.numpy as jnp
@@ -6,6 +7,14 @@
 from jax.sharding import PartitionSpec as P
 
 BLK_GRP = ("blk_0", "blk_1", "blk_2", "blk_3", "grp")
+
+
+def change_slots(a0, across):
+    odd = lax.all_gather(a0, across)
+    return jnp.concatenate(odd, axis=1)
+
+
+sector_divide = functools.partial(change_slots, across=BLK_GRP)
 
 
 def by_axis(array, axes):
@@ -33,7 +42,7 @@
         bar_count
     )
     zscores = (deviation * inverse).astype(jnp.bfloat16)
-    piece = lax.all_gather(zscores, BLK_GRP, axis=1, tiled=True)
+    piece = sector_divide(zscores)
     products = gram_tile(zscores, piece)
     column_block = jnp.arange(piece.shape[1], dtype=jnp.int32) // series_dev
     return jnp.where(column_block[None, :] >= my_index, products, jnp.float32(0.0)).astype(

time: 430 us -> 460 us (1.070)
  local copies, waits for them, and re-layouts: 0 us -> 44.1 us
  waiting for transfers between devices: 354 us -> 341 us
    reshape x0 -> x1, local copies, waits for them, and re-layouts: none -> 44.1 us  [change_slots(): return jnp.concatenate(odd, axis=1)]
    all_gather x1, waiting for transfers between devices: 354 us -> 341 us  [change_slots(): odd = lax.all_gather(a0, across)]
where the time goes in v1:
time: 460 us; the launch traced here: 459 us
  waiting for transfers between devices  341 us (74%)
  local copies, waits for them, and re-layouts  44.1 us (10%)
  blocking collectives  35.6 us (8%)
  matrix products  19.1 us (4%)
  between operations  13.4 us (3%)
  other arithmetic  5.51 us (1%)
    all_gather x1, waiting for transfers between devices, change_slots(): odd = lax.all_gather(a0, across)  341 us
    reshape x1, local copies, waits for them, and re-layouts, change_slots(): return jnp.concatenate(odd, axis=1)  44.1 us
    psum x5, blocking collectives, by_axis(): array = lax.psum(array, axis)  35.6 us
    dot_general x1, matrix products, gram_tile(): lax.dot_general(first, second, (((0,), (0,)), ((), ())), preferred_elemen...  19.1 us
  transfers between devices with their start and end apart: 1, of which 1 were waited for; matrix products, arithmetic and copies ran while one was open for 0% of the time, Pallas kernels for 0%

profile of v1, /device:TPU:1, one launch (start us, length us, event | category | flops | bytes accessed | tf_op | source)
XLA Modules:
  0.0 458.8 jit_solution(12013001140041439618)
XLA Ops:
  6.5 0.0 all-gather.3.cloned.1.call-start
  6.5 1.2 reduce_sum.27
  7.7 4.8 %psum.35 = f32[512]{0:T(512)S(1)} all-reduce(f32[512]{0:T(512)S(1)} %reduce_sum.27), channel_id=1, replica_groups=mesh['blk_0'=2,'blk_1'=4,'blk_2'=4,'blk_3'=2,'grp'=2] {'blk_0'}, use_global_device_ids=true, to_apply=%region_1.0 | all-reduce | flops 512 | bytes 4096 | tf_op jit(solution)/shard_map/psum | solution.py:22
  12.5 8.4 %psum.36 = f32[512]{0:T(512)S(1)} all-reduce(f32[512]{0:T(512)S(1)} %psum.35), channel_id=1, replica_groups=mesh['blk_0'=2,'blk_1'=4,'blk_2'=4,'blk_3'=2,'grp'=2] {'blk_1'}, use_global_device_ids=true, to_apply=%region_2.0 | all-reduce | flops 512 | bytes 4096 | tf_op jit(solution)/shard_map/psum | solution.py:22
  20.9 8.7 %psum.37 = f32[512]{0:T(512)S(1)} all-reduce(f32[512]{0:T(512)S(1)} %psum.36), channel_id=1, replica_groups=mesh['blk_0'=2,'blk_1'=4,'blk_2'=4,'blk_3'=2,'grp'=2] {'blk_2'}, use_global_device_ids=true, to_apply=%region_3.0 | all-reduce | flops 512 | bytes 4096 | tf_op jit(solution)/shard_map/psum | solution.py:22
  29.6 7.8 %psum.38 = f32[512]{0:T(512)S(1)} all-reduce(f32[512]{0:T(512)S(1)} %psum.37), channel_id=1, replica_groups=mesh['blk_0'=2,'blk_1'=4,'blk_2'=4,'blk_3'=2,'grp'=2] {'blk_3'}, use_global_device_ids=true, to_apply=%region_4.0 | all-reduce | flops 512 | bytes 4096 | tf_op jit(solution)/shard_map/psum | solution.py:22
  37.4 5.9 %psum.39 = f32[512]{0:T(512)S(1)} all-reduce(f32[512]{0:T(512)S(1)} %psum.38), channel_id=1, replica_groups=mesh['blk_0'=2,'blk_1'=4,'blk_2'=4,'blk_3'=2,'grp'=2] {'grp'}, use_global_device_ids=true, to_apply=%region_5.0 | all-reduce | flops 512 | bytes 4096 | tf_op jit(solution)/shard_map/psum | solution.py:22
  43.3 1.2 subtract_reduce_fusion
  44.5 1.2 multiply_reduce_fusion
  45.7 1.9 multiply_convert_fusion
  47.6 0.0 all-gather.3.cloned.1.call-update
  47.7 341.1 %all-gather.3.cloned.1.call-done = bf16[65536,256]{1,0:T(8,128)(2,1)} async-done(((bf16[512,256]{1,0:T(8,128)(2,1)}), bf16[65536,256]{1,0:T(8,128)(2,1)}) %all-gather.3.cloned.1.call-update) | async-done | bytes 33554448 | tf_op jit(solution)/shard_map/all_gather | solution.py:13
  388.8 0.0 copy-start
  388.8 44.1 %copy.2 = bf16[512,128,256]{0,2,1:T(8,128)(2,1)} copy(bf16[512,128,256]{2,0,1:T(8,128)(2,1)} %bitcast.6) | data formatting | bytes 67108864 | tf_op jit(solution)/shard_map/reshape | solution.py:14
  432.9 0.0 copy-done
  432.9 19.1 %fusion = bf16[256,32768]{1,0:T(8,128)(2,1)} fusion(bf16[512,256]{1,0:T(8,128)(2,1)S(1)} %copy-done, bf16[512,32768]{0,1:T(8,128)(2,1)} %bitcast.7, pred[32768]{0:T(1024)(128)(4,1)S(1)} %fusion.1), kind=kOutput, calls=%fused_computation.1 | convolution fusion | flops 8606711808 | bytes 50626560 | tf_op jit(solution)/shard_map/dot_general | solution.py:27
  (4 shorter events, 0.1 us)
Async XLA Ops:
  6.5 382.3 %all-gather.3.cloned.1.call-start = ((), (), s32[]{:S(2)}) async-start(), calls=%async_computation | async-start | bytes 33816576 | tf_op jit(solution)/shard_map/all_gather | solution.py:13
  388.8 44.1 %copy-start = (bf16[512,256]{1,0:T(8,128)(2,1)S(1)}, bf16[512,256]{1,0:T(8,128)(2,1)}, u32[]{:S(2)}) copy-start(bf16[512,256]{1,0:T(8,128)(2,1)} %multiply_convert_fusion) | copy-start | bytes 786436
Sparse Core Ops, SparseCore 0:
  47.8 340.9 all-gather.2
